TPU v7x, 32 devices: a 4x4x1 block of a 4x4x8 slice. The times are simulated.
32 devices in a mesh: dp: 2 (over z, core), tp: 16 (over x, y).
Axes of the slice: x: 4, y: 4, z: 1, core: 2. Of those that a mesh axis runs over, the one named last changes fastest.
The devices are a block of a 4x4x8 slice.
Arguments:
- x: bfloat16 [256, 3072], P('dp'), parts along dimension 0
- w_gate: bfloat16 [3072, 24576], P(None, 'tp')
- w_up: bfloat16 [3072, 24576], P(None, 'tp')
- w_down: bfloat16 [24576, 3072], P('tp')
Outputs:
- output: bfloat16 [256, 3072], P('dp'), parts along dimension 0
There are 2 independent parts. A program takes and returns all parts, laid end to end along the dimension named above; an argument that names none is the same for every part.
All inputs are finite; a program needn't handle non-finite values.
Results may differ from a plain program's by a relative error of at most 0.016.
Values are sent between devices in bfloat16 or wider.
A program may use at most 768 MiB of HBM per device.

v0:
```python
import jax
import jax.numpy as jnp
from jax import lax
from jax.sharding import PartitionSpec as P


def solution(mesh):
    def step(x, w_gate, w_up, w_down):
        gate = jnp.dot(x, w_gate, preferred_element_type=jnp.float32)
        up = jnp.dot(x, w_up, preferred_element_type=jnp.float32)
        hidden = (jax.nn.gelu(gate) * up).astype(jnp.bfloat16)
        term = jnp.dot(hidden, w_down, preferred_element_type=jnp.float32).astype(jnp.bfloat16)
        return lax.psum(term, "tp")

    return jax.shard_map(
        step,
        mesh=mesh,
        in_specs=(P("dp", None), P(None, "tp"), P(None, "tp"), P("tp", None)),
        out_specs=P("dp", None),
        check_vma=False,
    )
```

profile of v0, /device:TPU:96, one launch (start us, length us, event | category | flops | bytes accessed | tf_op | source)
XLA Modules:
  0.0 110.3 jit_solution(4888063423542800409)
XLA Ops:
  6.5 0.0 copy-start
  6.6 0.0 all-reduce.2.cloned.1.call-start
  6.6 1.1 %copy-done = bf16[128,3072]{1,0:T(8,128)(2,1)S(1)} copy-done((bf16[128,3072]{1,0:T(8,128)(2,1)S(1)}, bf16[128,3072]{1,0:T(8,128)(2,1)}, u32[]{:S(2)}) %copy-start) | copy-done | bytes 786456
  7.7 5.1 %fusion.16 = f32[128,1536]{1,0:T(8,128)S(1)} fusion(bf16[128,3072]{1,0:T(8,128)(2,1)S(1)} %copy-done, bf16[3072,1536]{1,0:T(8,128)(2,1)} %param.5), kind=kOutput, calls=%fused_computation.19 | convolution fusion | flops 1207959552 | bytes 11010048 | tf_op jit(solution)/shard_map/dot_general | solution.py:9
  12.8 10.1 %convolution_convert_fusion = bf16[128,3072]{1,0:T(8,128)(2,1)} fusion(bf16[1536,3072]{1,0:T(8,128)(2,1)} %param.7, bf16[128,3072]{1,0:T(8,128)(2,1)S(1)} %copy-done, bf16[3072,1536]{1,0:T(8,128)(2,1)} %param.6, f32[128,1536]{1,0:T(8,128)S(1)} %fusion.16), kind=kOutput, calls=%fused_computation | convolution fusion | flops 2418278400 | bytes 21233664 | tf_op jit(solution)/shard_map/dot_general | solution.py:12
  22.9 0.1 all-reduce.2.cloned.1.call-update
  23.0 78.4 %all-reduce.2.cloned.1.call-done = bf16[128,3072]{1,0:T(8,128)(2,1)} async-done(((bf16[128,3072]{1,0:T(8,128)(2,1)}), bf16[128,3072]{1,0:T(8,128)(2,1)}) %all-reduce.2.cloned.1.call-update) | async-done | bytes 786448 | tf_op jit(solution)/shard_map/psum | solution.py:13
  101.3 2.1 %copy.6 = bf16[128,3072]{1,0:T(8,128)(2,1)} copy(bf16[128,3072]{1,0:T(8,128)(2,1)} %all-reduce.2.cloned.1.call-done) | data formatting | bytes 1572864
Async XLA Ops:
  6.5 1.1 %copy-start = (bf16[128,3072]{1,0:T(8,128)(2,1)S(1)}, bf16[128,3072]{1,0:T(8,128)(2,1)}, u32[]{:S(2)}) copy-start(bf16[128,3072]{1,0:T(8,128)(2,1)} %param.4) | copy-start | bytes 2359300
  6.6 94.8 %all-reduce.2.cloned.1.call-start = ((), (), s32[]{:S(2)}) async-start(), calls=%async_computation | async-start | bytes 1572864 | tf_op jit(solution)/shard_map/psum | solution.py:13
Sparse Core Ops, SparseCore 0:
  23.1 78.2 all-reduce.1
where the time goes:
time: 111 us; the launch traced here: 110 us
  waiting for transfers between devices  78.4 us (71%)
  matrix products  15.2 us (14%)
  between operations  13.4 us (12%)
  local copies, waits for them, and re-layouts  3.19 us (3%)
    psum x1, waiting for transfers between devices, step(): return lax.psum(term, 'tp')  78.4 us
    dot_general x1, matrix products, step(): jnp.dot(hidden, w_down, preferred_element_type=jnp.float32)  10.1 us
    dot_general x1, matrix products, step(): gate = jnp.dot(x, w_gate, preferred_element_type=jnp.float32)  5.07 us
    unnamed x3, local copies, waits for them, and re-layouts  3.19 us
  transfers between devices with their start and end apart: 1, of which 1 were waited for; matrix products, arithmetic and copies ran while one was open for 0% of the time, Pallas kernels for 0%

commit v1 on v0

v1 whole, which is shorter than its diff:
```python
import functools
import math

import jax
import jax.numpy as jnp
from jax import lax
from jax.experimental import pallas as pl
from jax.experimental.pallas import tpu as pltpu
from jax.sharding import PartitionSpec as P

F32, BF16 = jnp.float32, jnp.bfloat16
MESH = pl.DeviceIdType.MESH
SLICES = 3
BLOCK = 256


def _kernel(side, x_hbm, wg_hbm, wu_hbm, wd_hbm, y, xv, wg, wu, wd, hid, term, send, part, psum, pout, p2, local_sem, ssem, rsem):
    me = lax.axis_index("tp")
    pos = (me // side, me % side)
    rows, depth = x_hbm.shape
    units = wg_hbm.shape[1]
    cw = send.shape[-1]
    span = side * cw
    quarter = rows // side

    def peer(axis, d):
        p = list(pos)
        p[axis] = lax.rem(p[axis] + d, side)
        return p[0] * side + p[1]

    barrier = pltpu.get_barrier_semaphore()
    for axis in (0, 1):
        for d in range(1, side):
            pl.semaphore_signal(barrier, inc=1, device_id={"tp": peer(axis, d)}, device_id_type=MESH)

    blocks = units // BLOCK
    cx = pltpu.make_async_copy(x_hbm, xv, local_sem.at[0])
    cx.start()
    cg, cu, cd = [], [], []
    for j in range(blocks):
        cols = pl.ds(j * BLOCK, BLOCK)
        cg.append(pltpu.make_async_copy(wg_hbm.at[:, cols], wg.at[j], local_sem.at[1 + j]))
        cu.append(pltpu.make_async_copy(wu_hbm.at[:, cols], wu.at[j], local_sem.at[1 + blocks + j]))
        cg[j].start()
        cu[j].start()
    for i in range(2 * SLICES):
        cd.append(pltpu.make_async_copy(wd_hbm.at[:, pl.ds(i * span, span)], wd.at[i], local_sem.at[1 + 2 * blocks + i]))
        cd[i].start()

    cx.wait()
    for j in range(blocks):
        cg[j].wait()
        gate = jnp.dot(xv[...], wg[j], preferred_element_type=F32)
        cu[j].wait()
        up = jnp.dot(xv[...], wu[j], preferred_element_type=F32)
        hid[:, j * BLOCK : (j + 1) * BLOCK] = (jax.nn.gelu(gate) * up).astype(BF16)

    def column(s, h, t):
        return pl.ds(pl.multiple_of((2 * s + h) * span + t * cw, cw), cw)

    def copy(stage, s, h, d, src, dst):
        axis = h if stage in (0, 3) else 1 - h
        i = ((s * 2 + h) * 4 + stage) * (side - 1) + d - 1
        return pltpu.make_async_remote_copy(
            src_ref=src,
            dst_ref=dst,
            send_sem=ssem.at[i],
            recv_sem=rsem.at[i],
            device_id={"tp": peer(axis, d)},
            device_id_type=MESH,
        )

    def copies(stage, s, h):
        mine, other = pos[h], pos[1 - h]
        out = []
        for d in range(1, side):
            if stage == 0:
                c = copy(0, s, h, d, send.at[s, h, lax.rem(mine + d, side)], part.at[s, h, d - 1])
            elif stage == 1:
                to = pl.multiple_of(lax.rem(other + d, side) * quarter, quarter)
                c = copy(1, s, h, d, pout.at[s, h, pl.ds(to, quarter)], p2.at[s, h, d - 1])
            elif stage == 2:
                block = y.at[pl.ds(pl.multiple_of(other * quarter, quarter), quarter), column(s, h, mine)]
                c = copy(2, s, h, d, block, block)
            else:
                block = y.at[:, column(s, h, mine)]
                c = copy(3, s, h, d, block, block)
            out.append(c)
        return out

    started = {}

    def start(stage, s, h):
        started[stage, s, h] = copies(stage, s, h)
        for c in started[stage, s, h]:
            c.start()

    for s in range(SLICES):
        for h in (0, 1):
            cd[2 * s + h].wait()
            t = jnp.dot(hid[...], wd[2 * s + h], preferred_element_type=F32)
            for k in range(side):
                piece = t[:, k * cw : (k + 1) * cw]
                term[s, h, k] = piece
                send[s, h, k] = piece.astype(BF16)
            if s == 0 and h == 0:
                pl.semaphore_wait(barrier, 2 * (side - 1))
            start(0, s, h)

    def advance(stage, s, h):
        for c in started[stage, s, h]:
            c.wait_recv()
        mine, other = pos[h], pos[1 - h]
        if stage == 0:
            total = term[s, h, mine]
            for d in range(side - 1):
                total = total + part[s, h, d].astype(F32)
            psum[s, h] = total
            pout[s, h] = total.astype(BF16)
            start(1, s, h)
        elif stage == 1:
            own = pl.ds(pl.multiple_of(other * quarter, quarter), quarter)
            total = psum[s, h, own, :]
            for d in range(side - 1):
                total = total + p2[s, h, d].astype(F32)
            y[own, column(s, h, mine)] = total.astype(BF16)
            start(2, s, h)
        elif stage == 2:
            start(3, s, h)

    for tick in range(SLICES + 3):
        for s in range(SLICES):
            if 0 <= tick - s < 4:
                for h in (0, 1):
                    advance(tick - s, s, h)
    for group in started.values():
        for c in group:
            c.wait_send()


def solution(mesh):
    side = math.isqrt(mesh.shape["tp"])

    def step(x, w_gate, w_up, w_down):
        rows, depth = x.shape
        units = w_gate.shape[1]
        cw = depth // (2 * SLICES * side)
        blocks = units // BLOCK
        quarter = rows // side
        count = SLICES * 2 * 4 * (side - 1)
        return pl.pallas_call(
            functools.partial(_kernel, side),
            out_shape=jax.ShapeDtypeStruct((rows, depth), BF16),
            in_specs=[pl.BlockSpec(memory_space=pltpu.HBM)] * 4,
            out_specs=pl.BlockSpec(memory_space=pltpu.VMEM),
            scratch_shapes=[
                pltpu.VMEM((rows, depth), BF16),
                pltpu.VMEM((blocks, depth, BLOCK), BF16),
                pltpu.VMEM((blocks, depth, BLOCK), BF16),
                pltpu.VMEM((2 * SLICES, units, side * cw), BF16),
                pltpu.VMEM((rows, units), BF16),
                pltpu.VMEM((SLICES, 2, side, rows, cw), F32),
                pltpu.VMEM((SLICES, 2, side, rows, cw), BF16),
                pltpu.VMEM((SLICES, 2, side - 1, rows, cw), BF16),
                pltpu.VMEM((SLICES, 2, rows, cw), F32),
                pltpu.VMEM((SLICES, 2, rows, cw), BF16),
                pltpu.VMEM((SLICES, 2, side - 1, quarter, cw), BF16),
                pltpu.SemaphoreType.DMA((1 + 2 * blocks + 2 * SLICES,)),
                pltpu.SemaphoreType.DMA((count,)),
                pltpu.SemaphoreType.DMA((count,)),
            ],
            compiler_params=pltpu.CompilerParams(
                collective_id=0, has_side_effects=True, vmem_limit_bytes=44 * 2**20
            ),
            name="mlp_block",
        )(*(pltpu.with_memory_space_constraint(a, pltpu.HBM) for a in (x, w_gate, w_up, w_down)))

    return jax.shard_map(
        step,
        mesh=mesh,
        in_specs=(P("dp", None), P(None, "tp"), P(None, "tp"), P("tp", None)),
        out_specs=P("dp", None),
        check_vma=False,
    )
```

time: 111 us -> 40.6 us (0.37)
  waiting for transfers between devices: 78.4 us -> 0 us
  Pallas kernels: 0 us -> 39.6 us
  matrix products: 15.2 us -> 0 us
  between operations: 13.4 us -> 0.01 us
  local copies, waits for them, and re-layouts: 3.19 us -> 0.88 us
    psum x1 -> x0, waiting for transfers between devices: 78.4 us -> none  [step(): return lax.psum(term, 'tp')]
    pallas_call x0 -> x1, Pallas kernels: none -> 39.6 us  [step(): pl.pallas_call(functools.partial(_kernel, side), out_shape=jax.ShapeDtype...]
    dot_general x2 -> x0, matrix products: 15.2 us -> none  [the longest x1 10.1 us: step(): jnp.dot(hidden, w_down, preferred_element_type=jnp.float32)]
    unnamed x3 -> x1, local copies, waits for them, and re-layouts: 3.19 us -> 0.88 us
  transfers between devices with their start and end apart: 1 -> 0, of which waited for: 1 -> 0; matrix products, arithmetic and copies ran while one was open for 0% -> 0% of each run, Pallas kernels for 0% -> 0%
where the time goes in v1:
time: 40.6 us; the launch traced here: 40.5 us
  Pallas kernels  39.6 us (98%)
  local copies, waits for them, and re-layouts  0.88 us (2%)
    pallas_call x1, Pallas kernels, step(): pl.pallas_call(functools.partial(_kernel, side), out_shape=jax.ShapeDtype...  39.6 us
    unnamed x1, local copies, waits for them, and re-layouts  0.88 us

profile of v1, /device:TPU:96, one launch (start us, length us, event | category | flops | bytes accessed | tf_op | source)
XLA Modules:
  0.0 40.5 jit_solution(1822095926021232519)
XLA Ops:
  0.0 39.6 %mlp_block.1 = bf16[128,3072]{1,0:T(8,128)(2,1)S(1)} custom-call(bf16[128,3072]{1,0:T(8,128)(2,1)} %x_hbm.1, bf16[3072,1536]{1,0:T(8,128)(2,1)} %wg_hbm.1, bf16[3072,1536]{1,0:T(8,128)(2,1)} %wu_hbm.1, bf16[1536,3072]{1,0:T(8,128)(2,1)} %wd_hbm.1), custom_call_target="tpu_custom_call" | custom-call | tf_op jit(solution)/shard_map/mlp_block/pallas_call | solution.py:151
  39.6 0.9 %copy.6 = bf16[128,3072]{1,0:T(8,128)(2,1)} copy(bf16[128,3072]{1,0:T(8,128)(2,1)S(1)} %mlp_block.1) | data formatting | bytes 1572864

commit v2 on v1

--- a/solution.py
+++ b/solution.py
@@ -128,11 +128,10 @@
         elif stage == 2:
             start(3, s, h)
 
-    for tick in range(SLICES + 3):
+    for stage in range(4):
         for s in range(SLICES):
-            if 0 <= tick - s < 4:
-                for h in (0, 1):
-                    advance(tick - s, s, h)
+            for h in (0, 1):
+                advance(stage, s, h)
     for group in started.values():
         for c in group:
             c.wait_send()

time: 40.6 us -> 33.3 us (0.82)
  Pallas kernels: 39.6 us -> 32.4 us
    pallas_call x1, Pallas kernels: 39.6 us -> 32.4 us  [step(): pl.pallas_call(functools.partial(_kernel, side), out_shape=jax.ShapeDtype...]
where the time goes in v2:
time: 33.3 us
  Pallas kernels  32.4 us (97%)
  local copies, waits for them, and re-layouts  0.88 us (3%)
    pallas_call x1, Pallas kernels, step(): pl.pallas_call(functools.partial(_kernel, side), out_shape=jax.ShapeDtype...  32.4 us
    unnamed x1, local copies, waits for them, and re-layouts  0.88 us

profile of v2, /device:TPU:96, one launch (start us, length us, event | category | flops | bytes accessed | tf_op | source)
XLA Modules:
  0.0 33.3 jit_solution(5984219189508351366)
XLA Ops:
  0.0 32.4 %mlp_block.1 = bf16[128,3072]{1,0:T(8,128)(2,1)S(1)} custom-call(bf16[128,3072]{1,0:T(8,128)(2,1)} %x_hbm.1, bf16[3072,1536]{1,0:T(8,128)(2,1)} %wg_hbm.1, bf16[3072,1536]{1,0:T(8,128)(2,1)} %wu_hbm.1, bf16[1536,3072]{1,0:T(8,128)(2,1)} %wd_hbm.1), custom_call_target="tpu_custom_call" | custom-call | tf_op jit(solution)/shard_map/mlp_block/pallas_call | solution.py:150
  32.4 0.9 %copy.6 = bf16[128,3072]{1,0:T(8,128)(2,1)} copy(bf16[128,3072]{1,0:T(8,128)(2,1)S(1)} %mlp_block.1) | data formatting | bytes 1572864

commit v3 on v0

v3 whole, which is shorter than its diff:
```python
import contextlib
import functools
import math

import jax
import jax.numpy as jnp
from jax import lax
from jax.experimental import pallas as pl
from jax.experimental.pallas import tpu as pltpu
from jax.sharding import PartitionSpec as P

F32, BF16 = jnp.float32, jnp.bfloat16
MESH = pl.DeviceIdType.MESH
BLOCK = 256
PIECE = 128
PARTS = 2


def scope(name):
    return contextlib.nullcontext()


def _kernel(side, x_hbm, wg_hbm, wu_hbm, wd_hbm, y, xv, wg, wu, wd, hid, acc, send, part, quad, outb, local_sem, xsem, hsem, ssem, rsem):
    dp, tp = lax.axis_index("dp"), lax.axis_index("tp")
    core = lax.rem(dp, 2)
    mate = dp + 1 - 2 * core
    pos = (tp // side, lax.rem(tp, side))
    rows = x_hbm.shape[0]
    blocks = wg.shape[0]
    half_units = blocks * BLOCK
    slices = wd.shape[1]
    span = side * PIECE
    high = rows // PARTS
    order = (2, 1, 3) if side == 4 else tuple(range(1, side))

    def peer(group, axis, d):
        p = list(pos)
        p[axis] = lax.rem(p[axis] + d, side)
        return {"dp": group, "tp": p[0] * side + p[1]}

    def remote(src, dst, send_sem, recv_sem, device):
        c = pltpu.make_async_remote_copy(
            src_ref=src, dst_ref=dst, send_sem=send_sem, recv_sem=recv_sem, device_id=device, device_id_type=MESH
        )
        c.start()

    def wait(ref, sem):
        pltpu.make_async_copy(ref, ref, sem).wait()

    barrier = pltpu.get_barrier_semaphore()
    others = [peer(dp, axis, d) for axis in (0, 1) for d in order] + [peer(mate, 1, d) for d in (0,) + order]
    for device in others:
        pl.semaphore_signal(barrier, inc=1, device_id=device, device_id_type=MESH)

    cx = pltpu.make_async_copy(x_hbm, xv.at[pl.ds(0, rows)], local_sem.at[0])
    cx.start()
    cg, cu, cd = [], [], {}
    for j in range(blocks):
        cols = pl.ds(pl.multiple_of(core * half_units + j * BLOCK, BLOCK), BLOCK)
        cg.append(pltpu.make_async_copy(wg_hbm.at[:, cols], wg.at[j], local_sem.at[1 + j]))
        cu.append(pltpu.make_async_copy(wu_hbm.at[:, cols], wu.at[j], local_sem.at[1 + blocks + j]))
        cg[j].start()
        cu[j].start()
    base = pl.multiple_of(core * slices * span, span)
    for k in (0, 1):
        units = pl.ds(pl.multiple_of((core if k == 0 else 1 - core) * half_units, BLOCK), half_units)
        for s in range(slices):
            cd[k, s] = pltpu.make_async_copy(
                wd_hbm.at[units, pl.ds(pl.multiple_of(base + s * span, span), span)],
                wd.at[k, s],
                local_sem.at[1 + 2 * blocks + k * slices + s],
            )
            cd[k, s].start()

    def hidden(j, first, count):
        at = pl.ds(first * rows, count * rows)
        gate = jnp.dot(xv[at], wg[j], preferred_element_type=F32)
        up = jnp.dot(xv[at], wu[j], preferred_element_type=F32)
        cols = pl.ds(j * BLOCK, BLOCK)
        hid[0, at, cols] = (jax.nn.gelu(gate) * up).astype(BF16)
        for g in range(first, first + count):
            remote(
                hid.at[0, pl.ds(g * rows, rows), cols],
                hid.at[1, pl.ds((1 - g) * rows, rows), cols],
                hsem.at[0],
                hsem.at[1],
                {"dp": mate, "tp": tp},
            )

    def loaded(j):
        with scope(f"gw{j}"):
            cg[j].wait()
            cu[j].wait()

    with scope("xw"):
        cx.wait()
    with scope("barw"):
        pl.semaphore_wait(barrier, len(others))
    remote(xv.at[pl.ds(0, rows)], xv.at[pl.ds(rows, rows)], xsem.at[0], xsem.at[1], {"dp": mate, "tp": tp})
    for j in range(blocks - 1):
        loaded(j)
        hidden(j, 0, 1)
    with scope("xrw"):
        wait(xv.at[pl.ds(rows, rows)], xsem.at[1])
    hidden(0, 1, 1)
    loaded(blocks - 1)
    hidden(blocks - 1, 0, 2)
    for j in range(1, blocks - 1):
        hidden(j, 1, 1)

    def column(s):
        return lambda t: pl.ds(pl.multiple_of(base + s * span + t * PIECE, PIECE), PIECE)

    def start(stage, u, h):
        s, r = u // PARTS, u % PARTS
        mine, other = pos[h], pos[1 - h]
        sem = rsem.at[(stage * slices * PARTS + u) * 2 + h]
        if stage == 0:
            for d in order:
                to = lax.rem(mine + d, side)
                remote(send.at[h, u, to], part.at[h, u, d - 1], ssem.at[0], sem, peer(dp, h, d))
        elif stage == 1:
            for d in order:
                remote(quad.at[h, u, other], quad.at[h, u, other], ssem.at[1], sem, peer(dp, 1 - h, d))
        else:
            block = y.at[pl.ds(r * high, high), column(s)(mine)]
            if h == 0:
                for d in order:
                    remote(block, block, ssem.at[2], sem, peer(dp, h, d))
            else:
                for d in order + (0,):
                    remote(outb.at[u], block, ssem.at[3], sem, peer(mate, h, d))

    for s in range(slices):
        with scope(f"dw0{s}"):
            cd[0, s].wait()
        acc[s] = jnp.dot(hid[0], wd[0, s], preferred_element_type=F32)
    with scope("hrw"):
        wait(hid.at[1], hsem.at[1])
    for s in range(slices):
        with scope(f"dw1{s}"):
            cd[1, s].wait()
        t = acc[s] + jnp.dot(hid[1], wd[1, s], preferred_element_type=F32)
        acc[s] = t
        for h in (0, 1):
            for r in range(PARTS):
                at = h * rows + r * high
                for k in range(side):
                    send[h, s * PARTS + r, k] = t[at : at + high, k * PIECE : (k + 1) * PIECE].astype(BF16)
        with scope(f"snd{s}"):
            for r in range(PARTS):
                for h in (0, 1):
                    start(0, s * PARTS + r, h)

    events = sorted((u + 7 * stage, u, stage) for u in range(slices * PARTS) for stage in range(3))
    for _, u, stage in events:
        s, r = u // PARTS, u % PARTS
        for h in (0, 1):
            mine, other = pos[h], pos[1 - h]
            with scope(f"rw{stage}_{u}{h}"):
                wait(quad.at[h, u] if stage == 2 and h == 1 else part.at[h, u], rsem.at[(stage * slices * PARTS + u) * 2 + h])
            if stage == 0:
                total = acc[s, pl.ds(h * rows + r * high, high), pl.ds(pl.multiple_of(mine * PIECE, PIECE), PIECE)]
                for d in range(side - 1):
                    total = total + part[h, u, d].astype(F32)
                quad[h, u, other] = total.astype(BF16)
                start(1, u, h)
            elif stage == 1:
                total = quad[h, u, 0].astype(F32)
                for k in range(1, side):
                    total = total + quad[h, u, k].astype(F32)
                if h == 0:
                    y[pl.ds(r * high, high), column(s)(mine)] = total.astype(BF16)
                else:
                    outb[u] = total.astype(BF16)
                start(2, u, h)
    with scope("sw"):
        wait(xv.at[pl.ds(0, rows)], xsem.at[0])
        wait(hid.at[0], hsem.at[0])
        wait(part, ssem.at[0])
        wait(part, ssem.at[1])
        wait(part.at[0], ssem.at[2])
        wait(quad.at[1], ssem.at[3])


def solution(mesh):
    side = math.isqrt(mesh.shape["tp"])

    def step(x, w_gate, w_up, w_down):
        rows, depth = x.shape
        half_units = w_gate.shape[1] // 2
        blocks = half_units // BLOCK
        slices = depth // (2 * side * PIECE)
        count = slices * PARTS
        high = rows // PARTS
        return pl.pallas_call(
            functools.partial(_kernel, side),
            out_shape=jax.ShapeDtypeStruct((rows, depth), BF16),
            in_specs=[pl.BlockSpec(memory_space=pltpu.HBM)] * 4,
            out_specs=pl.BlockSpec(memory_space=pltpu.VMEM),
            scratch_shapes=[
                pltpu.VMEM((2 * rows, depth), BF16),
                pltpu.VMEM((blocks, depth, BLOCK), BF16),
                pltpu.VMEM((blocks, depth, BLOCK), BF16),
                pltpu.VMEM((2, slices, half_units, side * PIECE), BF16),
                pltpu.VMEM((2, 2 * rows, half_units), BF16),
                pltpu.VMEM((slices, 2 * rows, side * PIECE), F32),
                pltpu.VMEM((2, count, side, high, PIECE), BF16),
                pltpu.VMEM((2, count, side - 1, high, PIECE), BF16),
                pltpu.VMEM((2, count, side, high, PIECE), BF16),
                pltpu.VMEM((count, high, PIECE), BF16),
                pltpu.SemaphoreType.DMA((1 + 2 * blocks + 2 * slices,)),
                pltpu.SemaphoreType.DMA((2,)),
                pltpu.SemaphoreType.DMA((2,)),
                pltpu.SemaphoreType.DMA((4,)),
                pltpu.SemaphoreType.DMA((3 * count * 2,)),
            ],
            compiler_params=pltpu.CompilerParams(
                collective_id=0, has_side_effects=True, vmem_limit_bytes=40 * 2**20
            ),
            name="mlp_block",
        )(*(pltpu.with_memory_space_constraint(a, pltpu.HBM) for a in (x, w_gate, w_up, w_down)))

    return jax.shard_map(
        step,
        mesh=mesh,
        in_specs=(P("dp", None), P(None, "tp"), P(None, "tp"), P("tp", None)),
        out_specs=P("dp", None),
        check_vma=False,
    )
```

time: 111 us -> 29.5 us (0.27)
  the two profiles are of different devices: /device:TPU:96 before, /device:TPU:97 now
where the time goes in v3:
time: 29.5 us; the launch traced here: 29.4 us
  Pallas kernels  28.5 us (97%)
  local copies, waits for them, and re-layouts  0.88 us (3%)
    pallas_call x1, Pallas kernels, step(): pl.pallas_call(functools.partial(_kernel, side), out_shape=jax.ShapeDtype...  28.5 us
    unnamed x1, local copies, waits for them, and re-layouts  0.88 us

profile of v3, /device:TPU:97, one launch (start us, length us, event | category | flops | bytes accessed | tf_op | source)
XLA Modules:
  0.0 29.4 jit_solution(9674309014134484453)
XLA Ops:
  0.0 28.5 %mlp_block.1 = bf16[128,3072]{1,0:T(8,128)(2,1)S(1)} custom-call(bf16[128,3072]{1,0:T(8,128)(2,1)} %x_hbm.1, bf16[3072,1536]{1,0:T(8,128)(2,1)} %wg_hbm.1, bf16[3072,1536]{1,0:T(8,128)(2,1)} %wu_hbm.1, bf16[1536,3072]{1,0:T(8,128)(2,1)} %wd_hbm.1), custom_call_target="tpu_custom_call" | custom-call | tf_op jit(solution)/shard_map/mlp_block/pallas_call | solution.py:196
  28.6 0.9 %copy.6 = bf16[128,3072]{1,0:T(8,128)(2,1)} copy(bf16[128,3072]{1,0:T(8,128)(2,1)S(1)} %mlp_block.1) | data formatting | bytes 1572864

commit v4 on v3

--- a/solution.py
+++ b/solution.py
@@ -48,7 +48,7 @@
         pltpu.make_async_copy(ref, ref, sem).wait()
 
     barrier = pltpu.get_barrier_semaphore()
-    others = [peer(dp, axis, d) for axis in (0, 1) for d in order] + [peer(mate, 1, d) for d in (0,) + order]
+    others = [peer(group, axis, d) for group in (dp, mate) for axis in (0, 1) for d in order] + [peer(mate, 0, 0)]
     for device in others:
         pl.semaphore_signal(barrier, inc=1, device_id=device, device_id_type=MESH)
 
@@ -72,91 +72,88 @@
             )
             cd[k, s].start()
 
-    def hidden(j, first, count):
-        at = pl.ds(first * rows, count * rows)
+    def hidden(j, g):
+        at, cols = pl.ds(g * rows, rows), pl.ds(j * BLOCK, BLOCK)
         gate = jnp.dot(xv[at], wg[j], preferred_element_type=F32)
         up = jnp.dot(xv[at], wu[j], preferred_element_type=F32)
-        cols = pl.ds(j * BLOCK, BLOCK)
         hid[0, at, cols] = (jax.nn.gelu(gate) * up).astype(BF16)
-        for g in range(first, first + count):
-            remote(
-                hid.at[0, pl.ds(g * rows, rows), cols],
-                hid.at[1, pl.ds((1 - g) * rows, rows), cols],
-                hsem.at[0],
-                hsem.at[1],
-                {"dp": mate, "tp": tp},
-            )
-
-    def loaded(j):
-        with scope(f"gw{j}"):
-            cg[j].wait()
-            cu[j].wait()
+
+    def share(j, g):
+        remote(
+            hid.at[0, pl.ds(g * rows, rows), pl.ds(j * BLOCK, BLOCK)],
+            hid.at[1, pl.ds((1 - g) * rows, rows), pl.ds(j * BLOCK, BLOCK)],
+            hsem.at[0],
+            hsem.at[1 + g],
+            {"dp": mate, "tp": tp},
+        )
 
     with scope("xw"):
         cx.wait()
     with scope("barw"):
         pl.semaphore_wait(barrier, len(others))
     remote(xv.at[pl.ds(0, rows)], xv.at[pl.ds(rows, rows)], xsem.at[0], xsem.at[1], {"dp": mate, "tp": tp})
-    for j in range(blocks - 1):
-        loaded(j)
-        hidden(j, 0, 1)
+    for j in range(blocks):
+        with scope(f"gw{j}"):
+            cg[j].wait()
+            cu[j].wait()
+        hidden(j, 0)
+        share(j, 0)
     with scope("xrw"):
         wait(xv.at[pl.ds(rows, rows)], xsem.at[1])
-    hidden(0, 1, 1)
-    loaded(blocks - 1)
-    hidden(blocks - 1, 0, 2)
-    for j in range(1, blocks - 1):
-        hidden(j, 1, 1)
+    for j in range(blocks):
+        hidden(j, 1)
+    for j in range(blocks):
+        share(j, 1)
 
     def column(s):
         return lambda t: pl.ds(pl.multiple_of(base + s * span + t * PIECE, PIECE), PIECE)
 
     def start(stage, u, h):
         s, r = u // PARTS, u % PARTS
-        mine, other = pos[h], pos[1 - h]
+        axis = (u + h) % 2
+        mine, other = pos[axis], pos[1 - axis]
         sem = rsem.at[(stage * slices * PARTS + u) * 2 + h]
         if stage == 0:
             for d in order:
                 to = lax.rem(mine + d, side)
-                remote(send.at[h, u, to], part.at[h, u, d - 1], ssem.at[0], sem, peer(dp, h, d))
+                remote(send.at[h, u, to], part.at[h, u, d - 1], ssem.at[0], sem, peer(dp, axis, d))
         elif stage == 1:
             for d in order:
-                remote(quad.at[h, u, other], quad.at[h, u, other], ssem.at[1], sem, peer(dp, 1 - h, d))
+                remote(quad.at[h, u, other], quad.at[h, u, other], ssem.at[1], sem, peer(dp, 1 - axis, d))
         else:
             block = y.at[pl.ds(r * high, high), column(s)(mine)]
             if h == 0:
                 for d in order:
-                    remote(block, block, ssem.at[2], sem, peer(dp, h, d))
+                    remote(block, block, ssem.at[2], sem, peer(dp, axis, d))
             else:
                 for d in order + (0,):
-                    remote(outb.at[u], block, ssem.at[3], sem, peer(mate, h, d))
-
-    for s in range(slices):
-        with scope(f"dw0{s}"):
-            cd[0, s].wait()
-        acc[s] = jnp.dot(hid[0], wd[0, s], preferred_element_type=F32)
-    with scope("hrw"):
-        wait(hid.at[1], hsem.at[1])
-    for s in range(slices):
-        with scope(f"dw1{s}"):
-            cd[1, s].wait()
-        t = acc[s] + jnp.dot(hid[1], wd[1, s], preferred_element_type=F32)
-        acc[s] = t
-        for h in (0, 1):
+                    remote(outb.at[u], block, ssem.at[3], sem, peer(mate, axis, d))
+
+    for h in (1, 0):
+        with scope(f"hrw{h}"):
+            wait(hid.at[0, pl.ds(0, rows)], hsem.at[2 - h])
+        at = pl.ds(h * rows, rows)
+        for s in range(slices):
+            if h == 1:
+                with scope(f"dw{s}"):
+                    cd[0, s].wait()
+                    cd[1, s].wait()
+            t = jnp.dot(hid[0, at], wd[0, s], preferred_element_type=F32)
+            t = t + jnp.dot(hid[1, at], wd[1, s], preferred_element_type=F32)
+            acc[s, at] = t
             for r in range(PARTS):
-                at = h * rows + r * high
                 for k in range(side):
-                    send[h, s * PARTS + r, k] = t[at : at + high, k * PIECE : (k + 1) * PIECE].astype(BF16)
-        with scope(f"snd{s}"):
-            for r in range(PARTS):
-                for h in (0, 1):
+                    piece = t[r * high : (r + 1) * high, k * PIECE : (k + 1) * PIECE]
+                    send[h, s * PARTS + r, k] = piece.astype(BF16)
+            with scope(f"snd{h}{s}"):
+                for r in range(PARTS):
                     start(0, s * PARTS + r, h)
 
-    events = sorted((u + 7 * stage, u, stage) for u in range(slices * PARTS) for stage in range(3))
-    for _, u, stage in events:
-        s, r = u // PARTS, u % PARTS
-        for h in (0, 1):
-            mine, other = pos[h], pos[1 - h]
+    for stage in range(3):
+        for h, u in [(h, u) for h in (1, 0) for u in range(slices * PARTS)]:
+            s, r = u // PARTS, u % PARTS
+            axis = (u + h) % 2
+            mine, other = pos[axis], pos[1 - axis]
             with scope(f"rw{stage}_{u}{h}"):
                 wait(quad.at[h, u] if stage == 2 and h == 1 else part.at[h, u], rsem.at[(stage * slices * PARTS + u) * 2 + h])
             if stage == 0:
@@ -211,7 +208,7 @@
                 pltpu.VMEM((count, high, PIECE), BF16),
                 pltpu.SemaphoreType.DMA((1 + 2 * blocks + 2 * slices,)),
                 pltpu.SemaphoreType.DMA((2,)),
-                pltpu.SemaphoreType.DMA((2,)),
+                pltpu.SemaphoreType.DMA((3,)),
                 pltpu.SemaphoreType.DMA((4,)),
                 pltpu.SemaphoreType.DMA((3 * count * 2,)),
             ],

time: 29.5 us -> 27.2 us (0.922)
  the two profiles are of different devices: /device:TPU:97 before, /device:TPU:96 now
where the time goes in v4:
time: 27.2 us; the launch traced here: 27.1 us
  Pallas kernels  26.2 us (96%)
  local copies, waits for them, and re-layouts  0.88 us (3%)
    pallas_call x1, Pallas kernels, step(): pl.pallas_call(functools.partial(_kernel, side), out_shape=jax.ShapeDtype...  26.2 us
    unnamed x1, local copies, waits for them, and re-layouts  0.88 us

profile of v4, /device:TPU:96, one launch (start us, length us, event | category | flops | bytes accessed | tf_op | source)
XLA Modules:
  0.0 27.1 jit_solution(5787068410592473457)
XLA Ops:
  0.0 26.2 %mlp_block.1 = bf16[128,3072]{1,0:T(8,128)(2,1)S(1)} custom-call(bf16[128,3072]{1,0:T(8,128)(2,1)} %x_hbm.1, bf16[3072,1536]{1,0:T(8,128)(2,1)} %wg_hbm.1, bf16[3072,1536]{1,0:T(8,128)(2,1)} %wu_hbm.1, bf16[1536,3072]{1,0:T(8,128)(2,1)} %wd_hbm.1), custom_call_target="tpu_custom_call" | custom-call | tf_op jit(solution)/shard_map/mlp_block/pallas_call | solution.py:193
  26.2 0.9 %copy.6 = bf16[128,3072]{1,0:T(8,128)(2,1)} copy(bf16[128,3072]{1,0:T(8,128)(2,1)S(1)} %mlp_block.1) | data formatting | bytes 1572864

commit v5 on v4

v5 whole, which is shorter than its diff:
```python
import contextlib
import functools
import math

import jax
import jax.numpy as jnp
from jax import lax
from jax.experimental import pallas as pl
from jax.experimental.pallas import tpu as pltpu
from jax.sharding import PartitionSpec as P

F32, BF16 = jnp.float32, jnp.bfloat16
MESH = pl.DeviceIdType.MESH
BLOCK = 256
PIECE = 128
PARTS = 2


def scope(name):
    return contextlib.nullcontext()


def _kernel(side, x_hbm, wg_hbm, wu_hbm, wd_hbm, y, xv, wgu, wd, hid, acc, send, part, quad, outb, local_sem, xsem, hsem, ssem, rsem):
    dp, tp = lax.axis_index("dp"), lax.axis_index("tp")
    core = lax.rem(dp, 2)
    mate = dp + 1 - 2 * core
    pos = (tp // side, lax.rem(tp, side))
    rows, depth = x_hbm.shape
    blocks = wgu.shape[0]
    half_units = blocks * BLOCK
    slices = wd.shape[1]
    span = side * PIECE
    high = rows // PARTS
    order = (2, 1, 3) if side == 4 else tuple(range(1, side))

    def peer(group, axis, d):
        p = list(pos)
        p[axis] = lax.rem(p[axis] + d, side)
        return {"dp": group, "tp": p[0] * side + p[1]}

    def remote(src, dst, send_sem, recv_sem, device):
        c = pltpu.make_async_remote_copy(
            src_ref=src, dst_ref=dst, send_sem=send_sem, recv_sem=recv_sem, device_id=device, device_id_type=MESH
        )
        c.start()

    def wait(ref, sem):
        pltpu.make_async_copy(ref, ref, sem).wait()

    barrier = pltpu.get_barrier_semaphore()
    others = [peer(group, axis, d) for group in (dp, mate) for axis in (0, 1) for d in order] + [peer(mate, 0, 0)]
    for device in others:
        pl.semaphore_signal(barrier, inc=1, device_id=device, device_id_type=MESH)

    cx = pltpu.make_async_copy(x_hbm, xv.at[pl.ds(0, rows)], local_sem.at[0])
    cx.start()
    for j in range(blocks):
        cols = pl.ds(pl.multiple_of(core * half_units + j * BLOCK, BLOCK), BLOCK)
        for k, w in enumerate((wg_hbm, wu_hbm)):
            load = pltpu.make_async_copy(w.at[:, cols], wgu.at[j, :, pl.ds(k * BLOCK, BLOCK)], local_sem.at[1 + j])
            load.start()
    base = pl.multiple_of(core * slices * span, span)
    for s in range(slices):
        for k in (0, 1):
            units = pl.ds(pl.multiple_of((core if k == 0 else 1 - core) * half_units, BLOCK), half_units)
            cols = pl.ds(pl.multiple_of(base + s * span, span), span)
            load = pltpu.make_async_copy(wd_hbm.at[units, cols], wd.at[k, s], local_sem.at[1 + blocks + s])
            load.start()

    def hidden(j, g):
        at, cols = pl.ds(g * rows, rows), pl.ds(j * BLOCK, BLOCK)
        both = jnp.dot(xv[at], wgu[j], preferred_element_type=F32)
        hid[0, at, cols] = (jax.nn.gelu(both[:, :BLOCK]) * both[:, BLOCK:]).astype(BF16)

    def share(j, g):
        remote(
            hid.at[0, pl.ds(g * rows, rows), pl.ds(j * BLOCK, BLOCK)],
            hid.at[1, pl.ds((1 - g) * rows, rows), pl.ds(j * BLOCK, BLOCK)],
            ssem,
            hsem.at[g],
            {"dp": mate, "tp": tp},
        )

    with scope("xw"):
        cx.wait()
    with scope("barw"):
        pl.semaphore_wait(barrier, len(others))
    remote(xv.at[pl.ds(0, rows)], xv.at[pl.ds(rows, rows)], ssem, xsem, {"dp": mate, "tp": tp})
    for j in range(blocks):
        with scope(f"gw{j}"):
            wait(wgu.at[j], local_sem.at[1 + j])
        hidden(j, 0)
        share(j, 0)
    with scope("xrw"):
        wait(xv.at[pl.ds(rows, rows)], xsem)
    for j in range(blocks):
        hidden(j, 1)
    for j in range(blocks):
        share(j, 1)

    def column(s):
        return lambda t: pl.ds(pl.multiple_of(base + s * span + t * PIECE, PIECE), PIECE)

    def start(stage, u, h):
        s, r = u // PARTS, u % PARTS
        axis = (u + h) % 2
        mine, other = pos[axis], pos[1 - axis]
        sem = rsem.at[min(stage * slices * PARTS + u, 2 * slices * PARTS) * 2 + (h if stage < 2 else 0)]
        if stage == 0:
            for d in order:
                to = lax.rem(mine + d, side)
                remote(send.at[h, u, to], part.at[h, u, d - 1], ssem, sem, peer(dp, axis, d))
        elif stage == 1:
            for d in order:
                remote(quad.at[h, u, other], quad.at[h, u, other], ssem, sem, peer(dp, 1 - axis, d))
        else:
            block = y.at[pl.ds(r * high, high), column(s)(mine)]
            if h == 0:
                for d in order:
                    remote(block, block, ssem, sem, peer(dp, axis, d))
            else:
                for d in order + (0,):
                    remote(outb.at[u], block, ssem, sem, peer(mate, axis, d))

    for h in (1, 0):
        with scope(f"hrw{h}"):
            wait(hid.at[0, pl.ds(0, rows)], hsem.at[1 - h])
        at = pl.ds(h * rows, rows)
        for s in range(slices):
            if h == 1:
                with scope(f"dw{s}"):
                    wait(wd.at[:, s], local_sem.at[1 + blocks + s])
            t = jnp.dot(hid[0, at], wd[0, s], preferred_element_type=F32)
            t = t + jnp.dot(hid[1, at], wd[1, s], preferred_element_type=F32)
            acc[s, at] = t
            for r in range(PARTS):
                for k in range(side):
                    piece = t[r * high : (r + 1) * high, k * PIECE : (k + 1) * PIECE]
                    send[h, s * PARTS + r, k] = piece.astype(BF16)
            with scope(f"snd{h}{s}"):
                for r in range(PARTS):
                    start(0, s * PARTS + r, h)

    for stage in range(2):
        for h, u in [(h, u) for h in (1, 0) for u in range(slices * PARTS)]:
            s, r = u // PARTS, u % PARTS
            axis = (u + h) % 2
            mine, other = pos[axis], pos[1 - axis]
            with scope(f"rw{stage}_{u}{h}"):
                wait(part.at[h, u], rsem.at[(stage * slices * PARTS + u) * 2 + h])
            if stage == 0:
                total = acc[s, pl.ds(h * rows + r * high, high), pl.ds(pl.multiple_of(mine * PIECE, PIECE), PIECE)]
                for d in range(side - 1):
                    total = total + part[h, u, d].astype(F32)
                quad[h, u, other] = total.astype(BF16)
                start(1, u, h)
            else:
                total = quad[h, u, 0].astype(F32)
                for k in range(1, side):
                    total = total + quad[h, u, k].astype(F32)
                if h == 0:
                    y[pl.ds(r * high, high), column(s)(mine)] = total.astype(BF16)
                else:
                    outb[u] = total.astype(BF16)
                start(2, u, h)
    pieces = slices * PARTS * high * PIECE
    taken = (2 * side - 1) * pieces
    with scope("ew"):
        wait(wd.at[:, :, pl.ds(0, taken // (2 * slices * span))], rsem.at[4 * slices * PARTS])
    given = 2 * rows * half_units + rows * depth + (4 * (side - 1) + 2 * side - 1) * pieces
    with scope("sw"):
        wait(wd.at[:, :, pl.ds(0, given // (2 * slices * span))], ssem)


def solution(mesh):
    side = math.isqrt(mesh.shape["tp"])

    def step(x, w_gate, w_up, w_down):
        rows, depth = x.shape
        half_units = w_gate.shape[1] // 2
        blocks = half_units // BLOCK
        slices = depth // (2 * side * PIECE)
        count = slices * PARTS
        high = rows // PARTS
        return pl.pallas_call(
            functools.partial(_kernel, side),
            out_shape=jax.ShapeDtypeStruct((rows, depth), BF16),
            in_specs=[pl.BlockSpec(memory_space=pltpu.HBM)] * 4,
            out_specs=pl.BlockSpec(memory_space=pltpu.VMEM),
            scratch_shapes=[
                pltpu.VMEM((2 * rows, depth), BF16),
                pltpu.VMEM((blocks, depth, 2 * BLOCK), BF16),
                pltpu.VMEM((2, slices, half_units, side * PIECE), BF16),
                pltpu.VMEM((2, 2 * rows, half_units), BF16),
                pltpu.VMEM((slices, 2 * rows, side * PIECE), F32),
                pltpu.VMEM((2, count, side, high, PIECE), BF16),
                pltpu.VMEM((2, count, side - 1, high, PIECE), BF16),
                pltpu.VMEM((2, count, side, high, PIECE), BF16),
                pltpu.VMEM((count, high, PIECE), BF16),
                pltpu.SemaphoreType.DMA((1 + blocks + slices,)),
                pltpu.SemaphoreType.DMA,
                pltpu.SemaphoreType.DMA((2,)),
                pltpu.SemaphoreType.DMA,
                pltpu.SemaphoreType.DMA((4 * count + 1,)),
            ],
            compiler_params=pltpu.CompilerParams(
                collective_id=0, has_side_effects=True, vmem_limit_bytes=40 * 2**20
            ),
            name="mlp_block",
        )(*(pltpu.with_memory_space_constraint(a, pltpu.HBM) for a in (x, w_gate, w_up, w_down)))

    return jax.shard_map(
        step,
        mesh=mesh,
        in_specs=(P("dp", None), P(None, "tp"), P(None, "tp"), P("tp", None)),
        out_specs=P("dp", None),
        check_vma=False,
    )
```

time: 27.2 us -> 27 us (level)
  no operation moved by 1% of the time
where the time goes in v5:
time: 27 us; the launch traced here: 26.9 us
  Pallas kernels  26 us (96%)
  local copies, waits for them, and re-layouts  0.88 us (3%)
    pallas_call x1, Pallas kernels, step(): pl.pallas_call(functools.partial(_kernel, side), out_shape=jax.ShapeDtype...  26 us
    unnamed x1, local copies, waits for them, and re-layouts  0.88 us

profile of v5, /device:TPU:96, one launch (start us, length us, event | category | flops | bytes accessed | tf_op | source)
XLA Modules:
  0.0 26.9 jit_solution(7262250824235372029)
XLA Ops:
  0.0 26.0 %mlp_block.1 = bf16[128,3072]{1,0:T(8,128)(2,1)S(1)} custom-call(bf16[128,3072]{1,0:T(8,128)(2,1)} %x_hbm.1, bf16[3072,1536]{1,0:T(8,128)(2,1)} %wg_hbm.1, bf16[3072,1536]{1,0:T(8,128)(2,1)} %wu_hbm.1, bf16[1536,3072]{1,0:T(8,128)(2,1)} %wd_hbm.1), custom_call_target="tpu_custom_call" | custom-call | tf_op jit(solution)/shard_map/mlp_block/pallas_call | solution.py:185
  26.0 0.9 %copy.6 = bf16[128,3072]{1,0:T(8,128)(2,1)} copy(bf16[128,3072]{1,0:T(8,128)(2,1)S(1)} %mlp_block.1) | data formatting | bytes 1572864

commit v6 on v5

--- a/solution.py
+++ b/solution.py
@@ -20,7 +20,7 @@
     return contextlib.nullcontext()
 
 
-def _kernel(side, x_hbm, wg_hbm, wu_hbm, wd_hbm, y, xv, wgu, wd, hid, acc, send, part, quad, outb, local_sem, xsem, hsem, ssem, rsem):
+def _kernel(side, x_hbm, wg_hbm, wu_hbm, wd_hbm, y, xv, wgu, first, wd, hid, acc, send, part, quad, outb, local_sem, xsem, hsem, ssem, rsem):
     dp, tp = lax.axis_index("dp"), lax.axis_index("tp")
     core = lax.rem(dp, 2)
     mate = dp + 1 - 2 * core
@@ -54,23 +54,32 @@
 
     cx = pltpu.make_async_copy(x_hbm, xv.at[pl.ds(0, rows)], local_sem.at[0])
     cx.start()
-    for j in range(blocks):
+    deep = (pl.ds(0, depth // 2), pl.ds(depth // 2, depth // 2))
+    loads = [(j, pl.ds(0, depth)) for j in range(blocks - 1)] + [(blocks - 1, deep[0]), (blocks - 1, deep[1])]
+    for n, (j, at) in enumerate(loads):
         cols = pl.ds(pl.multiple_of(core * half_units + j * BLOCK, BLOCK), BLOCK)
         for k, w in enumerate((wg_hbm, wu_hbm)):
-            load = pltpu.make_async_copy(w.at[:, cols], wgu.at[j, :, pl.ds(k * BLOCK, BLOCK)], local_sem.at[1 + j])
+            load = pltpu.make_async_copy(w.at[at, cols], wgu.at[j, at, pl.ds(k * BLOCK, BLOCK)], local_sem.at[1 + n])
             load.start()
     base = pl.multiple_of(core * slices * span, span)
     for s in range(slices):
         for k in (0, 1):
             units = pl.ds(pl.multiple_of((core if k == 0 else 1 - core) * half_units, BLOCK), half_units)
             cols = pl.ds(pl.multiple_of(base + s * span, span), span)
-            load = pltpu.make_async_copy(wd_hbm.at[units, cols], wd.at[k, s], local_sem.at[1 + blocks + s])
+            load = pltpu.make_async_copy(wd_hbm.at[units, cols], wd.at[k, s], local_sem.at[2 + blocks + s])
             load.start()
 
-    def hidden(j, g):
-        at, cols = pl.ds(g * rows, rows), pl.ds(j * BLOCK, BLOCK)
-        both = jnp.dot(xv[at], wgu[j], preferred_element_type=F32)
-        hid[0, at, cols] = (jax.nn.gelu(both[:, :BLOCK]) * both[:, BLOCK:]).astype(BF16)
+    def finish(j, g, both):
+        hidden = jax.nn.gelu(both[:, :BLOCK]) * both[:, BLOCK:]
+        hid[0, pl.ds(g * rows, rows), pl.ds(j * BLOCK, BLOCK)] = hidden.astype(BF16)
+
+    def product(j, g, at):
+        return jnp.dot(xv[pl.ds(g * rows, rows), at], wgu[j, at], preferred_element_type=F32)
+
+    def loaded(n):
+        j, at = loads[n]
+        with scope(f"gw{n}"):
+            wait(wgu.at[j, at], local_sem.at[1 + n])
 
     def share(j, g):
         remote(
@@ -81,20 +90,31 @@
             {"dp": mate, "tp": tp},
         )
 
+    whole = pl.ds(0, depth)
     with scope("xw"):
         cx.wait()
     with scope("barw"):
         pl.semaphore_wait(barrier, len(others))
-    remote(xv.at[pl.ds(0, rows)], xv.at[pl.ds(rows, rows)], ssem, xsem, {"dp": mate, "tp": tp})
-    for j in range(blocks):
-        with scope(f"gw{j}"):
-            wait(wgu.at[j], local_sem.at[1 + j])
-        hidden(j, 0)
+    mine, theirs = pl.ds(0, rows), pl.ds(rows, rows)
+    for k in (0, 1):
+        remote(xv.at[mine, deep[k]], xv.at[theirs, deep[k]], ssem, xsem.at[k], {"dp": mate, "tp": tp})
+    for j in range(blocks - 1):
+        loaded(j)
+        finish(j, 0, product(j, 0, whole))
         share(j, 0)
-    with scope("xrw"):
-        wait(xv.at[pl.ds(rows, rows)], xsem)
-    for j in range(blocks):
-        hidden(j, 1)
+    loaded(blocks - 1)
+    first[...] = product(blocks - 1, 0, deep[0])
+    loaded(blocks)
+    finish(blocks - 1, 0, first[...] + product(blocks - 1, 0, deep[1]))
+    share(blocks - 1, 0)
+    with scope("xrw0"):
+        wait(xv.at[theirs, deep[0]], xsem.at[0])
+    first[...] = product(0, 1, deep[0])
+    with scope("xrw1"):
+        wait(xv.at[theirs, deep[1]], xsem.at[1])
+    finish(0, 1, first[...] + product(0, 1, deep[1]))
+    for j in range(1, blocks):
+        finish(j, 1, product(j, 1, whole))
     for j in range(blocks):
         share(j, 1)
 
@@ -129,7 +149,7 @@
         for s in range(slices):
             if h == 1:
                 with scope(f"dw{s}"):
-                    wait(wd.at[:, s], local_sem.at[1 + blocks + s])
+                    wait(wd.at[:, s], local_sem.at[2 + blocks + s])
             t = jnp.dot(hid[0, at], wd[0, s], preferred_element_type=F32)
             t = t + jnp.dot(hid[1, at], wd[1, s], preferred_element_type=F32)
             acc[s, at] = t
@@ -190,6 +210,7 @@
             scratch_shapes=[
                 pltpu.VMEM((2 * rows, depth), BF16),
                 pltpu.VMEM((blocks, depth, 2 * BLOCK), BF16),
+                pltpu.VMEM((rows, 2 * BLOCK), F32),
                 pltpu.VMEM((2, slices, half_units, side * PIECE), BF16),
                 pltpu.VMEM((2, 2 * rows, half_units), BF16),
                 pltpu.VMEM((slices, 2 * rows, side * PIECE), F32),
@@ -197,8 +218,8 @@
                 pltpu.VMEM((2, count, side - 1, high, PIECE), BF16),
                 pltpu.VMEM((2, count, side, high, PIECE), BF16),
                 pltpu.VMEM((count, high, PIECE), BF16),
-                pltpu.SemaphoreType.DMA((1 + blocks + slices,)),
-                pltpu.SemaphoreType.DMA,
+                pltpu.SemaphoreType.DMA((2 + blocks + slices,)),
+                pltpu.SemaphoreType.DMA((2,)),
                 pltpu.SemaphoreType.DMA((2,)),
                 pltpu.SemaphoreType.DMA,
                 pltpu.SemaphoreType.DMA((4 * count + 1,)),

time: 27 us -> 26.8 us (level)
  no operation moved by 1% of the time
where the time goes in v6:
time: 26.8 us; the launch traced here: 26.7 us
  Pallas kernels  25.9 us (97%)
  local copies, waits for them, and re-layouts  0.88 us (3%)
    pallas_call x1, Pallas kernels, step(): pl.pallas_call(functools.partial(_kernel, side), out_shape=jax.ShapeDtype...  25.9 us
    unnamed x1, local copies, waits for them, and re-layouts  0.88 us

profile of v6, /device:TPU:96, one launch (start us, length us, event | category | flops | bytes accessed | tf_op | source)
XLA Modules:
  0.0 26.7 jit_solution(12039777742913429352)
XLA Ops:
  0.0 25.9 %mlp_block.1 = bf16[128,3072]{1,0:T(8,128)(2,1)S(1)} custom-call(bf16[128,3072]{1,0:T(8,128)(2,1)} %x_hbm.1, bf16[3072,1536]{1,0:T(8,128)(2,1)} %wg_hbm.1, bf16[3072,1536]{1,0:T(8,128)(2,1)} %wu_hbm.1, bf16[1536,3072]{1,0:T(8,128)(2,1)} %wd_hbm.1), custom_call_target="tpu_custom_call" | custom-call | tf_op jit(solution)/shard_map/mlp_block/pallas_call | solution.py:205
  25.9 0.9 %copy.6 = bf16[128,3072]{1,0:T(8,128)(2,1)} copy(bf16[128,3072]{1,0:T(8,128)(2,1)S(1)} %mlp_block.1) | data formatting | bytes 1572864

commit v7 on v6

--- a/solution.py
+++ b/solution.py
@@ -81,10 +81,10 @@
         with scope(f"gw{n}"):
             wait(wgu.at[j, at], local_sem.at[1 + n])
 
-    def share(j, g):
+    def share(j, g, n=1):
         remote(
-            hid.at[0, pl.ds(g * rows, rows), pl.ds(j * BLOCK, BLOCK)],
-            hid.at[1, pl.ds((1 - g) * rows, rows), pl.ds(j * BLOCK, BLOCK)],
+            hid.at[0, pl.ds(g * rows, rows), pl.ds(j * BLOCK, n * BLOCK)],
+            hid.at[1, pl.ds((1 - g) * rows, rows), pl.ds(j * BLOCK, n * BLOCK)],
             ssem,
             hsem.at[g],
             {"dp": mate, "tp": tp},
@@ -115,8 +115,7 @@
     finish(0, 1, first[...] + product(0, 1, deep[1]))
     for j in range(1, blocks):
         finish(j, 1, product(j, 1, whole))
-    for j in range(blocks):
-        share(j, 1)
+    share(0, 1, blocks)
 
     def column(s):
         return lambda t: pl.ds(pl.multiple_of(base + s * span + t * PIECE, PIECE), PIECE)
@@ -152,14 +151,13 @@
                     wait(wd.at[:, s], local_sem.at[2 + blocks + s])
             t = jnp.dot(hid[0, at], wd[0, s], preferred_element_type=F32)
             t = t + jnp.dot(hid[1, at], wd[1, s], preferred_element_type=F32)
-            acc[s, at] = t
             for r in range(PARTS):
                 for k in range(side):
                     piece = t[r * high : (r + 1) * high, k * PIECE : (k + 1) * PIECE]
                     send[h, s * PARTS + r, k] = piece.astype(BF16)
-            with scope(f"snd{h}{s}"):
-                for r in range(PARTS):
+                with scope(f"snd{h}{s}{r}"):
                     start(0, s * PARTS + r, h)
+            acc[s, at] = t
 
     for stage in range(2):
         for h, u in [(h, u) for h in (1, 0) for u in range(slices * PARTS)]:

time: 26.8 us -> 26.8 us (level)
  no operation moved by 1% of the time
where the time goes in v7:
time: 26.8 us; the launch traced here: 26.7 us
  Pallas kernels  25.8 us (96%)
  local copies, waits for them, and re-layouts  0.88 us (3%)
    pallas_call x1, Pallas kernels, step(): pl.pallas_call(functools.partial(_kernel, side), out_shape=jax.ShapeDtype...  25.8 us
    unnamed x1, local copies, waits for them, and re-layouts  0.88 us

profile of v7, /device:TPU:96, one launch (start us, length us, event | category | flops | bytes accessed | tf_op | source)
XLA Modules:
  0.0 26.7 jit_solution(13458979270388383830)
XLA Ops:
  0.0 25.8 %mlp_block.1 = bf16[128,3072]{1,0:T(8,128)(2,1)S(1)} custom-call(bf16[128,3072]{1,0:T(8,128)(2,1)} %x_hbm.1, bf16[3072,1536]{1,0:T(8,128)(2,1)} %wg_hbm.1, bf16[3072,1536]{1,0:T(8,128)(2,1)} %wu_hbm.1, bf16[1536,3072]{1,0:T(8,128)(2,1)} %wd_hbm.1), custom_call_target="tpu_custom_call" | custom-call | tf_op jit(solution)/shard_map/mlp_block/pallas_call | solution.py:203
  25.8 0.9 %copy.6 = bf16[128,3072]{1,0:T(8,128)(2,1)} copy(bf16[128,3072]{1,0:T(8,128)(2,1)S(1)} %mlp_block.1) | data formatting | bytes 1572864

commit v8 on v7

--- a/solution.py
+++ b/solution.py
@@ -48,14 +48,16 @@
         pltpu.make_async_copy(ref, ref, sem).wait()
 
     barrier = pltpu.get_barrier_semaphore()
-    others = [peer(group, axis, d) for group in (dp, mate) for axis in (0, 1) for d in order] + [peer(mate, 0, 0)]
+    others = [peer(mate, 0, 0)] + [peer(group, axis, d) for d in order for group in (mate, dp) for axis in (0, 1)]
     for device in others:
         pl.semaphore_signal(barrier, inc=1, device_id=device, device_id_type=MESH)
 
     cx = pltpu.make_async_copy(x_hbm, xv.at[pl.ds(0, rows)], local_sem.at[0])
     cx.start()
     deep = (pl.ds(0, depth // 2), pl.ds(depth // 2, depth // 2))
-    loads = [(j, pl.ds(0, depth)) for j in range(blocks - 1)] + [(blocks - 1, deep[0]), (blocks - 1, deep[1])]
+    cut = depth * 7 // 12
+    late = (pl.ds(0, cut), pl.ds(cut, depth - cut))
+    loads = [(j, pl.ds(0, depth)) for j in range(blocks - 1)] + [(blocks - 1, late[0]), (blocks - 1, late[1])]
     for n, (j, at) in enumerate(loads):
         cols = pl.ds(pl.multiple_of(core * half_units + j * BLOCK, BLOCK), BLOCK)
         for k, w in enumerate((wg_hbm, wu_hbm)):
@@ -103,9 +105,9 @@
         finish(j, 0, product(j, 0, whole))
         share(j, 0)
     loaded(blocks - 1)
-    first[...] = product(blocks - 1, 0, deep[0])
+    first[...] = product(blocks - 1, 0, late[0])
     loaded(blocks)
-    finish(blocks - 1, 0, first[...] + product(blocks - 1, 0, deep[1]))
+    finish(blocks - 1, 0, first[...] + product(blocks - 1, 0, late[1]))
     share(blocks - 1, 0)
     with scope("xrw0"):
         wait(xv.at[theirs, deep[0]], xsem.at[0])

time: 26.8 us -> 26.8 us (level)
  no operation moved by 1% of the time
where the time goes in v8:
time: 26.8 us; the launch traced here: 26.7 us
  Pallas kernels  25.8 us (96%)
  local copies, waits for them, and re-layouts  0.88 us (3%)
    pallas_call x1, Pallas kernels, step(): pl.pallas_call(functools.partial(_kernel, side), out_shape=jax.ShapeDtype...  25.8 us
    unnamed x1, local copies, waits for them, and re-layouts  0.88 us

profile of v8, /device:TPU:96, one launch (start us, length us, event | category | flops | bytes accessed | tf_op | source)
XLA Modules:
  0.0 26.7 jit_solution(18376900778384684912)
XLA Ops:
  0.0 25.8 %mlp_block.1 = bf16[128,3072]{1,0:T(8,128)(2,1)S(1)} custom-call(bf16[128,3072]{1,0:T(8,128)(2,1)} %x_hbm.1, bf16[3072,1536]{1,0:T(8,128)(2,1)} %wg_hbm.1, bf16[3072,1536]{1,0:T(8,128)(2,1)} %wu_hbm.1, bf16[1536,3072]{1,0:T(8,128)(2,1)} %wd_hbm.1), custom_call_target="tpu_custom_call" | custom-call | tf_op jit(solution)/shard_map/mlp_block/pallas_call | solution.py:205
  25.8 0.9 %copy.6 = bf16[128,3072]{1,0:T(8,128)(2,1)} copy(bf16[128,3072]{1,0:T(8,128)(2,1)S(1)} %mlp_block.1) | data formatting | bytes 1572864

commit v9 on v8

--- a/solution.py
+++ b/solution.py
@@ -124,9 +124,9 @@
 
     def start(stage, u, h):
         s, r = u // PARTS, u % PARTS
-        axis = (u + h) % 2
+        axis = (u + h + 1) % 2
         mine, other = pos[axis], pos[1 - axis]
-        sem = rsem.at[min(stage * slices * PARTS + u, 2 * slices * PARTS) * 2 + (h if stage < 2 else 0)]
+        sem = rsem.at[min(stage * slices + s, 2 * slices) * 2 + (h if stage < 2 else 0)]
         if stage == 0:
             for d in order:
                 to = lax.rem(mine + d, side)
@@ -164,10 +164,11 @@
     for stage in range(2):
         for h, u in [(h, u) for h in (1, 0) for u in range(slices * PARTS)]:
             s, r = u // PARTS, u % PARTS
-            axis = (u + h) % 2
+            axis = (u + h + 1) % 2
             mine, other = pos[axis], pos[1 - axis]
-            with scope(f"rw{stage}_{u}{h}"):
-                wait(part.at[h, u], rsem.at[(stage * slices * PARTS + u) * 2 + h])
+            if r == 0:
+                with scope(f"rw{stage}_{s}{h}"):
+                    wait(part.at[h, pl.ds(u, PARTS)], rsem.at[(stage * slices + s) * 2 + h])
             if stage == 0:
                 total = acc[s, pl.ds(h * rows + r * high, high), pl.ds(pl.multiple_of(mine * PIECE, PIECE), PIECE)]
                 for d in range(side - 1):
@@ -186,7 +187,7 @@
     pieces = slices * PARTS * high * PIECE
     taken = (2 * side - 1) * pieces
     with scope("ew"):
-        wait(wd.at[:, :, pl.ds(0, taken // (2 * slices * span))], rsem.at[4 * slices * PARTS])
+        wait(wd.at[:, :, pl.ds(0, taken // (2 * slices * span))], rsem.at[4 * slices])
     given = 2 * rows * half_units + rows * depth + (4 * (side - 1) + 2 * side - 1) * pieces
     with scope("sw"):
         wait(wd.at[:, :, pl.ds(0, given // (2 * slices * span))], ssem)
@@ -222,7 +223,7 @@
                 pltpu.SemaphoreType.DMA((2,)),
                 pltpu.SemaphoreType.DMA((2,)),
                 pltpu.SemaphoreType.DMA,
-                pltpu.SemaphoreType.DMA((4 * count + 1,)),
+                pltpu.SemaphoreType.DMA((4 * slices + 1,)),
             ],
             compiler_params=pltpu.CompilerParams(
                 collective_id=0, has_side_effects=True, vmem_limit_bytes=40 * 2**20

time: 26.8 us -> 26.8 us (level)
  no operation moved by 1% of the time
where the time goes in v9:
time: 26.8 us; the launch traced here: 26.7 us
  Pallas kernels  25.8 us (96%)
  local copies, waits for them, and re-layouts  0.88 us (3%)
    pallas_call x1, Pallas kernels, step(): pl.pallas_call(functools.partial(_kernel, side), out_shape=jax.ShapeDtype...  25.8 us
    unnamed x1, local copies, waits for them, and re-layouts  0.88 us

profile of v9, /device:TPU:96, one launch (start us, length us, event | category | flops | bytes accessed | tf_op | source)
XLA Modules:
  0.0 26.7 jit_solution(11412538766853328361)
XLA Ops:
  0.0 25.8 %mlp_block.1 = bf16[128,3072]{1,0:T(8,128)(2,1)S(1)} custom-call(bf16[128,3072]{1,0:T(8,128)(2,1)} %x_hbm.1, bf16[3072,1536]{1,0:T(8,128)(2,1)} %wg_hbm.1, bf16[3072,1536]{1,0:T(8,128)(2,1)} %wu_hbm.1, bf16[1536,3072]{1,0:T(8,128)(2,1)} %wd_hbm.1), custom_call_target="tpu_custom_call" | custom-call | tf_op jit(solution)/shard_map/mlp_block/pallas_call | solution.py:206
  25.8 0.9 %copy.6 = bf16[128,3072]{1,0:T(8,128)(2,1)} copy(bf16[128,3072]{1,0:T(8,128)(2,1)S(1)} %mlp_block.1) | data formatting | bytes 1572864
